TPU v7x, 128 devices: a whole 4x4x4 slice. The times are simulated.
128 devices in a mesh: lat: 4 (over x), ord: 16 (over y, z), batch: 2 (over core).
Axes of the slice: x: 4, y: 4, z: 4, core: 2. Of those that a mesh axis runs over, the one named last changes fastest.
Arguments:
- state_field: bfloat16 [512, 720, 1440], P(('batch', 'ord'), 'lat'), parts along dimension 0, may hold values from -6 to 6
- slot_order: int32 [512], replicated, may hold values from 0 to 511, each once
- legendre: bfloat16 [512, 720, 720], P(('lat', 'ord')), may hold values from -0.21875 to 0.21875
- degree_gain: float32 [720, 256], replicated, may hold values from 0.25 to 1.75
- mixing: bfloat16 [256, 256], replicated, may hold values from -0.375 to 0.375
Outputs:
- updated: bfloat16 [512, 720, 1440], P(('batch', 'ord'), 'lat'), parts along dimension 0
There are 2 independent parts, one for each index of `batch`. A program takes and returns all parts, laid end to end along the dimension named above; an argument that names none is the same for every part. Nothing has to cross between parts.
Inputs may be any that keep to these rules, and one draw needn't show every extreme that they name: `slot_order`: each of 0 to 511 stands once.
All inputs are finite; a program needn't handle non-finite values.
Results may differ from a plain program's by a relative error of at most 0.0054.
Values may be sent and summed in bfloat16 or wider, within the bound.
A program may use at most 192 MiB of HBM per device.

v0:
```python
import math
import jax
import jax.numpy as jnp
from jax import lax
from jax.sharding import PartitionSpec as P


def tables(orders, lon_count):
    longitude = jnp.arange(lon_count, dtype=jnp.int32)
    phase = orders[:, None] * longitude[None, :] % lon_count
    angle = phase.astype(jnp.float32) * (2.0 * math.pi / lon_count)
    root = 1.0 / math.sqrt(lon_count)
    cosine = jnp.cos(angle)
    sine = jnp.sin(angle)
    forward = jnp.stack([cosine * root, -sine * root], axis=1).astype(jnp.bfloat16)
    weights = jnp.where(orders == 0, 1.0, 2.0).astype(jnp.float32) * root
    inverse = jnp.stack([cosine * weights[:, None], -sine * weights[:, None]], axis=1).astype(
        jnp.bfloat16
    )
    return (forward, inverse)


def shards(state_field, slot_order, legendre, degree_gain, mixing):
    channels, lat_rows, lon_count = state_field.shape
    all_slots = slot_order.shape[0]
    my_slots, degrees, latitudes = legendre.shape
    width = mixing.shape[0]
    lat_count = lax.axis_size("lat")
    ord_count = lax.axis_size("ord")
    forward, inverse = tables(slot_order, lon_count)
    fourier = lax.dot_general(
        forward.reshape(2 * all_slots, lon_count),
        state_field.reshape(channels * lat_rows, lon_count),
        (((1,), (1,)), ((), ())),
        preferred_element_type=jnp.float32,
    )
    fourier = fourier.astype(jnp.bfloat16)
    arrived = lax.all_to_all(
        fourier.reshape(1, all_slots, 2, channels, lat_rows),
        ("lat", "ord"),
        split_axis=1,
        concat_axis=0,
        tiled=True,
    )
    arrived = arrived.reshape(lat_count, ord_count, my_slots, 2, channels, lat_rows).transpose(
        2, 3, 1, 4, 0, 5
    )
    gathered = arrived.reshape(my_slots, 2 * width, latitudes)
    orders_here = lax.dynamic_slice_in_dim(
        slot_order, lax.axis_index(("lat", "ord")) * my_slots, my_slots, 0
    )
    padded_gain = jnp.concatenate([degree_gain, jnp.zeros((degrees, width), jnp.float32)], axis=0)
    spec = jnp.einsum("sjl,sxl->sjx", legendre, gathered, preferred_element_type=jnp.float32)

    def pick_rows(order_value):
        return lax.dynamic_slice_in_dim(padded_gain, order_value, degrees, 0)

    gain_rows = jax.vmap(pick_rows)(orders_here)
    kept = jnp.arange(degrees, dtype=jnp.int32)[None, :] < (degrees - orders_here)[:, None]
    filtered = jnp.where(
        kept[:, :, None, None],
        spec.reshape(my_slots, degrees, 2, width) * gain_rows[:, :, None, :],
        0.0,
    )
    filtered = filtered.astype(jnp.bfloat16)
    mixed = jnp.dot(
        filtered.reshape(my_slots * degrees * 2, width), mixing, preferred_element_type=jnp.float32
    )
    mixed = mixed.astype(jnp.bfloat16).reshape(my_slots, degrees, 2 * width)
    synth = jnp.einsum("sjx,sjl->sxl", mixed, legendre, preferred_element_type=jnp.float32).astype(
        jnp.bfloat16
    )
    outgoing = synth.reshape(my_slots, 2, ord_count, channels, lat_count, lat_rows).transpose(
        4, 2, 0, 1, 3, 5
    )
    outgoing = outgoing.reshape(lat_count * ord_count, my_slots, 2, channels, lat_rows)
    returned = lax.all_to_all(outgoing, ("lat", "ord"), split_axis=0, concat_axis=0, tiled=True)
    returned = returned.reshape(2 * all_slots, channels * lat_rows)
    back = lax.dot_general(
        returned,
        inverse.reshape(2 * all_slots, lon_count),
        (((0,), (0,)), ((), ())),
        preferred_element_type=jnp.float32,
    )
    back = back.reshape(channels, lat_rows, lon_count)
    return (state_field.astype(jnp.float32) + jax.nn.gelu(back, approximate=True)).astype(
        jnp.bfloat16
    )


def solution(mesh):
    placed = (P(("batch", "ord"), "lat", None), P(), P(("lat", "ord"), None, None), P(), P())
    return jax.shard_map(
        shards,
        mesh=mesh,
        in_specs=placed,
        out_specs=P(("batch", "ord"), "lat", None),
        check_vma=False,
    )
```

profile of v0, /device:TPU:82, one launch (start us, length us, event | category | flops | bytes accessed | tf_op | source)
XLA Modules:
  0.0 555.3 jit_solution(5158348730062671081)
XLA Ops:
  0.0 0.7 select_multiply_fusion
  0.7 14.0 %multiply_convert_fusion.1 = (bf16[512,1,1440]{0,2,1:T(8,128)(2,1)S(1)}, bf16[512,1,1440]{0,2,1:T(8,128)(2,1)S(1)}, bf16[512,1,1440]{0,2,1:T(8,128)(2,1)S(1)}, bf16[512,1,1440]{0,2,1:T(8,128)(2,1)S(1)}) fusion(f32[512]{0:T(512)S(1)} %select_multiply_fusion, s32[512]{0:T(512)} %param.6), kind=kLoop, calls=%fused_computation.28 | loop fusion | flops 13271040 | bytes 5902336 | tf_op jit(solution)/shard_map/convert
  14.7 2.9 pad_maximum_fusion
  17.6 7.4 %copy.33 = bf16[512,2,1440]{2,1,0:T(2,128)(2,1)S(1)} copy(bf16[512,2,1440]{0,2,1:T(8,128)(2,1)} %get-tuple-element.27) | data formatting | bytes 5898240 | tf_op jit(solution)/shard_map/stack | solution.py:15
  25.0 3.6 convert_element_type.65
  28.6 11.9 %copy.34 = bf16[16,180,1440]{2,1,0:T(8,128)(2,1)} copy(bf16[16,180,1440]{2,0,1:T(8,128)(2,1)} %param.5) | data formatting | bytes 16588800 | tf_op args[0]
  40.5 10.9 %reshape.240 = bf16[2880,1440]{1,0:T(8,128)(2,1)} reshape(bf16[16,180,1440]{2,1,0:T(8,128)(2,1)} %copy.34) | data formatting | bytes 16588800 | tf_op jit(solution)/shard_map/reshape | solution.py:33
  51.4 13.7 %convolution_convert_fusion.1 = bf16[1024,2880]{0,1:T(8,128)(2,1)} fusion(bf16[1024,1440]{1,0:T(8,128)(2,1)S(1)} %copy-done.2, bf16[2880,1440]{1,0:T(8,128)(2,1)} %reshape.240), kind=kOutput, calls=%fused_computation.17 | convolution fusion | flops 8496414720 | bytes 17141760 | tf_op jit(solution)/shard_map/dot_general | solution.py:31
  65.1 8.5 %copy.35 = bf16[1024,2880]{1,0:T(8,128)(2,1)} copy(bf16[1024,2880]{0,1:T(8,128)(2,1)} %convolution_convert_fusion.1) | data formatting | bytes 11796480 | tf_op jit(solution)/shard_map/convert_element_type | solution.py:37
  73.6 27.5 %reshape.241 = bf16[1,512,2,16,180]{4,3,2,1,0:T(8,128)(2,1)} reshape(bf16[1024,2880]{1,0:T(8,128)(2,1)} %copy.35) | data formatting | bytes 11796480 | tf_op jit(solution)/shard_map/reshape | solution.py:39
  101.1 11.5 %all-to-all-start = ((bf16[1,512,2,16,180]{4,3,2,0,1:T(8,128)(2,1)}), bf16[1,512,2,16,180]{4,3,2,0,1:T(8,128)(2,1)}, u32[]{:S(2)}, u32[]{:S(2)}) async-start(bf16[1,512,2,16,180]{4,3,2,0,1:T(8,128)(2,1)} %bitcast.34), calls=%async_computation | async-start | bytes 16777216 | tf_op jit(solution)/shard_map/all_to_all | solution.py:38
  112.5 0.8 broadcast_subtract_fusion
  113.3 0.1 concatenate.6
  113.4 17.8 %while.1 = (s32[]{:T(128)}, f32[1440,256]{1,0:T(8,128)S(1)}, s32[8,2]{0,1:T(2,128)S(1)}, f32[8,720,256]{2,1,0:T(8,128)}, s32[]{:T(128)}) while((s32[]{:T(128)}, f32[1440,256]{1,0:T(8,128)S(1)}, s32[8,2]{0,1:T(2,128)S(1)}, f32[8,720,256]{2,1,0:T(8,128)}, s32[]{:T(128)}) %tuple.21), condition=%wide.while_cond, body=%wide.while_body.sunk | while | flops 2 | bytes 1475173 | solution.py:56
  113.4 0.1 constant_dynamic-slice_fusion.2
  113.5 0.6 slice.12
  114.1 1.6 bitcast_dynamic-update-slice_fusion.2
  115.7 0.1 constant_dynamic-slice_fusion.2
  115.7 0.6 slice.12
  116.3 1.6 bitcast_dynamic-update-slice_fusion.2
  117.9 0.1 constant_dynamic-slice_fusion.2
  118.0 0.6 slice.12
  118.6 1.6 bitcast_dynamic-update-slice_fusion.2
  120.1 0.1 constant_dynamic-slice_fusion.2
  120.2 0.6 slice.12
  120.8 1.6 bitcast_dynamic-update-slice_fusion.2
  122.4 0.1 constant_dynamic-slice_fusion.2
  122.4 0.6 slice.12
  123.0 1.6 bitcast_dynamic-update-slice_fusion.2
  124.6 0.1 constant_dynamic-slice_fusion.2
  124.6 0.6 slice.12
  125.2 1.6 bitcast_dynamic-update-slice_fusion.2
  126.8 0.1 constant_dynamic-slice_fusion.2
  126.9 0.6 slice.12
  127.4 1.6 bitcast_dynamic-update-slice_fusion.2
  129.0 0.1 constant_dynamic-slice_fusion.2
  129.1 0.6 slice.12
  129.7 1.6 bitcast_dynamic-update-slice_fusion.2
  131.3 13.0 %mul.158 = f32[8,720,2,256]{3,2,1,0:T(2,128)} broadcast(f32[8,720,256]{2,1,0:T(8,128)} %get-tuple-element.12), dimensions={0,1,3} | broadcast | bytes 17694720 | tf_op jit(solution)/shard_map/mul | solution.py:62
  144.3 14.9 %mul.159 = f32[11520,256]{1,0:T(8,128)} reshape(f32[8,720,2,256]{3,2,1,0:T(2,128)} %mul.158) | data formatting | bytes 23592960 | tf_op jit(solution)/shard_map/mul | solution.py:62
  159.2 0.1 iota_compare_fusion
  159.3 1.5 broadcast_in_dim.36
  160.7 2.4 broadcast_in_dim.37
  163.2 71.0 %all-to-all-done = bf16[1,512,2,16,180]{4,3,2,0,1:T(8,128)(2,1)} async-done(((bf16[1,512,2,16,180]{4,3,2,0,1:T(8,128)(2,1)}), bf16[1,512,2,16,180]{4,3,2,0,1:T(8,128)(2,1)}, u32[]{:S(2)}, u32[]{:S(2)}) %all-to-all-start) | async-done | bytes 5898272 | tf_op jit(solution)/shard_map/all_to_all | solution.py:38
  234.1 12.1 %copy.56 = bf16[4,16,8,2,16,180]{5,0,4,1,3,2:T(4,128)(2,1)} copy(bf16[4,16,8,2,16,180]{5,4,3,2,1,0:T(8,128)(2,1)} %bitcast.1) | data formatting | bytes 11796480 | tf_op jit(solution)/shard_map/reshape | solution.py:45
  246.3 15.3 %reshape.243 = bf16[8,512,720]{2,1,0:T(8,128)(2,1)} reshape(bf16[8,2,16,16,4,180]{5,4,3,2,1,0:T(4,128)(2,1)} %bitcast.35) | data formatting | bytes 11796480 | tf_op jit(solution)/shard_map/reshape | solution.py:48
  261.5 14.4 %convolution_bitcast_fusion = f32[8,720,512]{2,1,0:T(8,128)} fusion(bf16[8,512,720]{2,1,0:T(8,128)(2,1)} %reshape.243, bf16[8,720,720]{2,1,0:T(8,128)(2,1)} %param.7), kind=kOutput, calls=%fused_computation.19 | convolution fusion | flops 4246732800 | bytes 25989120 | tf_op jit(solution)/shard_map/sjl,sxl->sjx/dot_general | solution.py:53
  276.0 13.5 %reshape.244 = f32[11520,256]{1,0:T(8,128)} reshape(f32[8,720,512]{2,1,0:T(8,128)} %convolution_bitcast_fusion) | data formatting | bytes 23592960 | tf_op jit(solution)/shard_map/reshape | solution.py:62
  289.5 13.4 %convolution_convert_fusion = bf16[11520,256]{1,0:T(8,128)(2,1)} fusion(bf16[256,256]{1,0:T(8,128)(2,1)S(1)} %copy-done, f32[11520,256]{1,0:T(8,128)} %reshape.244, f32[11520,256]{1,0:T(8,128)} %mul.159, pred[11520]{0:T(1024)(128)(4,1)S(1)} %broadcast_in_dim.37), kind=kOutput, calls=%fused_computation.12 | convolution fusion | flops 1521745920 | bytes 29633792 | tf_op jit(solution)/shard_map/dot_general | solution.py:66
  302.9 9.7 %reshape.245 = bf16[8,720,512]{2,1,0:T(8,128)(2,1)} reshape(bf16[11520,256]{1,0:T(8,128)(2,1)} %convolution_convert_fusion) | data formatting | bytes 11796480 | tf_op jit(solution)/shard_map/reshape | solution.py:69
  312.6 11.8 %convolution_convert_fusion.2 = bf16[8,512,720]{1,2,0:T(8,128)(2,1)} fusion(bf16[8,720,512]{2,1,0:T(8,128)(2,1)} %reshape.245, bf16[8,720,720]{2,1,0:T(8,128)(2,1)} %param.7), kind=kOutput, calls=%fused_computation.20 | convolution fusion | flops 4249681920 | bytes 20090880 | tf_op jit(solution)/shard_map/sjx,sjl->sxl/dot_general | solution.py:70
  324.4 8.4 %copy.40 = bf16[8,512,720]{2,1,0:T(8,128)(2,1)} copy(bf16[8,512,720]{1,2,0:T(8,128)(2,1)} %convolution_convert_fusion.2) | data formatting | bytes 11796480 | tf_op jit(solution)/shard_map/convert_element_type | solution.py:70
  332.9 18.0 %reshape.246 = bf16[8,2,16,16,4,180]{5,4,3,2,1,0:T(4,128)(2,1)} reshape(bf16[8,512,720]{2,1,0:T(8,128)(2,1)} %copy.40) | data formatting | bytes 11796480 | tf_op jit(solution)/shard_map/reshape | solution.py:73
  350.9 8.2 %copy.41 = bf16[4,16,8,2,16,180]{5,4,3,2,1,0:T(8,128)(2,1)} copy(bf16[4,16,8,2,16,180]{5,0,4,1,3,2:T(4,128)(2,1)} %bitcast.36) | data formatting | bytes 11796480 | tf_op jit(solution)/shard_map/transpose | solution.py:73
  359.2 9.6 %all-to-all-start.1 = ((bf16[64,8,2,16,180]{4,3,2,1,0:T(8,128)(2,1)}), bf16[64,8,2,16,180]{4,3,2,1,0:T(8,128)(2,1)}, u32[]{:S(2)}, u32[]{:S(2)}) async-start(bf16[64,8,2,16,180]{4,3,2,1,0:T(8,128)(2,1)} %bitcast.37), calls=%async_computation.1 | async-start | bytes 16777216 | tf_op jit(solution)/shard_map/all_to_all | solution.py:77
  368.8 7.4 %copy.43 = bf16[512,2,1440]{2,1,0:T(2,128)(2,1)S(1)} copy(bf16[512,2,1440]{0,2,1:T(8,128)(2,1)} %get-tuple-element.28) | data formatting | bytes 5898240 | tf_op jit(solution)/shard_map/stack | solution.py:17
  376.2 3.5 convert_element_type.70
  379.7 111.8 %all-to-all-done.1 = bf16[64,8,2,16,180]{4,3,2,1,0:T(8,128)(2,1)} async-done(((bf16[64,8,2,16,180]{4,3,2,1,0:T(8,128)(2,1)}), bf16[64,8,2,16,180]{4,3,2,1,0:T(8,128)(2,1)}, u32[]{:S(2)}, u32[]{:S(2)}) %all-to-all-start.1) | async-done | bytes 5898272 | tf_op jit(solution)/shard_map/all_to_all | solution.py:77
  491.5 15.6 %reshape.248 = bf16[1024,2880]{1,0:T(8,128)(2,1)} reshape(bf16[64,8,2,16,180]{4,3,2,1,0:T(8,128)(2,1)} %all-to-all-done.1) | data formatting | bytes 11796480 | tf_op jit(solution)/shard_map/reshape | solution.py:78
  507.1 8.4 %copy.42 = bf16[2880,1024]{1,0:T(8,128)(2,1)} copy(bf16[2880,1024]{0,1:T(8,128)(2,1)} %bitcast.38) | data formatting | bytes 11796480 | tf_op jit(solution)/shard_map/dot_general | solution.py:79
  515.5 8.0 %dot_general.27 = bf16[16,180,1024]{2,1,0:T(8,128)(2,1)} reshape(bf16[2880,1024]{1,0:T(8,128)(2,1)} %copy.42) | data formatting | bytes 11796480 | tf_op jit(solution)/shard_map/dot_general | solution.py:79
  523.5 16.3 %fusion.11 = f32[16,180,1440]{2,1,0:T(8,128)} fusion(bf16[16,180,1024]{2,1,0:T(8,128)(2,1)} %dot_general.27, bf16[1024,1440]{1,0:T(8,128)(2,1)} %convert_element_type.70), kind=kOutput, calls=%fused_computation.21 | convolution fusion | flops 8493465600 | bytes 25436160 | tf_op jit(solution)/shard_map/dot_general | solution.py:79
  539.8 0.0 copy-start.1
  539.8 15.3 %fusion.8 = bf16[16,180,1440]{2,0,1:T(8,128)(2,1)} fusion(f32[16,180,1440]{2,1,0:T(8,128)} %fusion.11, bf16[16,180,1440]{2,0,1:T(8,128)(2,1)S(1)} %bitcast.33), kind=kLoop, calls=%fused_computation.11 | loop fusion | flops 45619200 | bytes 33177600 | tf_op jit(solution)/shard_map/convert_element_type | solution.py:86
  (16 shorter events, 0.0 us)
Async XLA Ops:
  0.0 289.5 %copy-start = (bf16[256,256]{1,0:T(8,128)(2,1)S(1)}, bf16[256,256]{1,0:T(8,128)(2,1)}, u32[]{:S(2)}) copy-start(bf16[256,256]{1,0:T(8,128)(2,1)} %param.9) | copy-start | bytes 393220
  40.5 10.9 %copy-start.2 = (bf16[1024,1440]{1,0:T(8,128)(2,1)S(1)}, bf16[1024,1440]{1,0:T(8,128)(2,1)}, u32[]{:S(2)}) copy-start(bf16[1024,1440]{1,0:T(8,128)(2,1)} %convert_element_type.65) | copy-start | bytes 8847364
  101.1 12.3 %copy-start.3 = (f32[720,256]{1,0:T(8,128)S(1)}, f32[720,256]{1,0:T(8,128)}, u32[]{:S(2)}) copy-start(f32[720,256]{1,0:T(8,128)} %param.8) | copy-start | bytes 2211844
  101.1 133.1 %all-to-all-start = ((bf16[1,512,2,16,180]{4,3,2,0,1:T(8,128)(2,1)}), bf16[1,512,2,16,180]{4,3,2,0,1:T(8,128)(2,1)}, u32[]{:S(2)}, u32[]{:S(2)}) async-start(bf16[1,512,2,16,180]{4,3,2,0,1:T(8,128)(2,1)} %bitcast.34), calls=%async_computation | async-start | bytes 16777216 | tf_op jit(solution)/shard_map/all_to_all | solution.py:38
  359.2 132.4 %all-to-all-start.1 = ((bf16[64,8,2,16,180]{4,3,2,1,0:T(8,128)(2,1)}), bf16[64,8,2,16,180]{4,3,2,1,0:T(8,128)(2,1)}, u32[]{:S(2)}, u32[]{:S(2)}) async-start(bf16[64,8,2,16,180]{4,3,2,1,0:T(8,128)(2,1)} %bitcast.37), calls=%async_computation.1 | async-start | bytes 16777216 | tf_op jit(solution)/shard_map/all_to_all | solution.py:77
  515.5 24.3 %slice-start = ((s8[8847360]{0:T(1024)(128)(4,1)}), s8[458752]{0:T(1024)(128)(4,1)S(1)}, s32[]{:S(2)}) async-start(s8[8847360]{0:T(1024)(128)(4,1)} %bitcast.32), calls=%async_computation.2 | async-start | bytes 917504
  523.5 16.3 %slice-start.1 = ((s8[8847360]{0:T(1024)(128)(4,1)}), s8[4194304]{0:T(1024)(128)(4,1)S(1)}, s32[]{:S(2)}) async-start(s8[8847360]{0:T(1024)(128)(4,1)} %bitcast.32), calls=%async_computation.3 | async-start | bytes 8388608
  523.5 16.3 %slice-start.2 = ((s8[8847360]{0:T(1024)(128)(4,1)}), s8[4194304]{0:T(1024)(128)(4,1)S(1)}, s32[]{:S(2)}) async-start(s8[8847360]{0:T(1024)(128)(4,1)} %bitcast.32), calls=%async_computation.4 | async-start | bytes 8388608
  539.8 15.3 %copy-start.1 = (bf16[256,256]{1,0:T(8,128)(2,1)S(1)}, bf16[256,256]{1,0:T(8,128)(2,1)}, u32[]{:S(2)}) copy-start(bf16[256,256]{1,0:T(8,128)(2,1)} %param.9) | copy-start | bytes 393220
where the time goes:
time: 565 us; the launch traced here: 555 us
  local copies, waits for them, and re-layouts  248 us (44%)
  waiting for transfers between devices  183 us (32%)
  matrix products  69.6 us (12%)
  other arithmetic  33.7 us (6%)
  starting transfers between devices  21 us (4%)
    all_to_all x1, waiting for transfers between devices, shards(): lax.all_to_all(outgoing, ('lat', 'ord'), split_axis=0, concat_axis=0, til...  112 us
    all_to_all x1, waiting for transfers between devices, shards(): lax.all_to_all(fourier.reshape(1, all_slots, 2, channels, lat_rows), ('la...  71 us
    mul x2, local copies, waits for them, and re-layouts, shards(): spec.reshape(my_slots, degrees, 2, width) * gain_rows[:, :, None, :]  27.9 us
    reshape x1, local copies, waits for them, and re-layouts, shards(): fourier.reshape(1, all_slots, 2, channels, lat_rows)  27.5 us
    reshape x1, local copies, waits for them, and re-layouts, shards(): synth.reshape(my_slots, 2, ord_count, channels, lat_count, lat_rows)  18 us
    gather x24, local copies, waits for them, and re-layouts  17.8 us
    dot_general x2, local copies, waits for them, and re-layouts, shards(): lax.dot_general(returned, inverse.reshape(2 * all_slots, lon_count), (((0...  16.4 us
    dot_general x1, matrix products, shards(): lax.dot_general(returned, inverse.reshape(2 * all_slots, lon_count), (((0...  16.3 us
  transfers between devices with their start and end apart: 2, of which 2 were waited for; matrix products, arithmetic and copies ran while one was open for 11% of the time, Pallas kernels for 0%

commit v1 on v0

--- a/solution.py
+++ b/solution.py
@@ -35,12 +35,20 @@
         preferred_element_type=jnp.float32,
     )
     fourier = fourier.astype(jnp.bfloat16)
-    arrived = lax.all_to_all(
-        fourier.reshape(1, all_slots, 2, channels, lat_rows),
-        ("lat", "ord"),
-        split_axis=1,
-        concat_axis=0,
-        tiled=True,
+    arrived = jnp.concatenate(
+        lax.all_to_all(
+            jnp.stack(
+                jnp.split(
+                    fourier.reshape(1, all_slots, 2, channels, lat_rows),
+                    lax.axis_size(("lat", "ord")),
+                    axis=1,
+                )
+            ),
+            ("lat", "ord"),
+            0,
+            0,
+        ),
+        axis=0,
     )
     arrived = arrived.reshape(lat_count, ord_count, my_slots, 2, channels, lat_rows).transpose(
         2, 3, 1, 4, 0, 5

time: 565 us -> 667 us (1.18)
  local copies, waits for them, and re-layouts: 248 us -> 346 us
    unnamed x15 -> x78, local copies, waits for them, and re-layouts: 11.9 us -> 110 us
    another operation x0 -> x2, local copies, waits for them, and re-layouts: none -> 13.7 us  [the longest x1 12.1 us: shards(): arrived.reshape(lat_count, ord_count, my_slots, 2, channels, lat_rows)]
    reshape x1 -> x0, local copies, waits for them, and re-layouts: 12.1 us -> none  [shards(): arrived.reshape(lat_count, ord_count, my_slots, 2, channels, lat_rows)]
  transfers between devices with their start and end apart: 2 -> 2, of which waited for: 2 -> 2; matrix products, arithmetic and copies ran while one was open for 11% -> 9% of each run, Pallas kernels for 0% -> 0%
where the time goes in v1:
time: 667 us; the launch traced here: 655 us
  local copies, waits for them, and re-layouts  346 us (52%)
  waiting for transfers between devices  184 us (28%)
  matrix products  69.9 us (10%)
  other arithmetic  33.7 us (5%)
  starting transfers between devices  20.7 us (3%)
    all_to_all x1, waiting for transfers between devices, shards(): lax.all_to_all(outgoing, ('lat', 'ord'), split_axis=0, concat_axis=0, til...  112 us
    unnamed x78, local copies, waits for them, and re-layouts  110 us
    all_to_all x1, waiting for transfers between devices, shards(): lax.all_to_all(jnp.stack(jnp.split(fourier.reshape(1, all_slots, 2, chann...  72.6 us
    mul x2, local copies, waits for them, and re-layouts, shards(): spec.reshape(my_slots, degrees, 2, width) * gain_rows[:, :, None, :]  27.9 us
    reshape x1, local copies, waits for them, and re-layouts, shards(): fourier.reshape(1, all_slots, 2, channels, lat_rows)  27.5 us
    reshape x1, local copies, waits for them, and re-layouts, shards(): synth.reshape(my_slots, 2, ord_count, channels, lat_count, lat_rows)  18 us
    dot_general x2, local copies, waits for them, and re-layouts, shards(): lax.dot_general(returned, inverse.reshape(2 * all_slots, lon_count), (((0...  16.4 us
    dot_general x1, matrix products, shards(): lax.dot_general(returned, inverse.reshape(2 * all_slots, lon_count), (((0...  16.3 us
  transfers between devices with their start and end apart: 2, of which 2 were waited for; matrix products, arithmetic and copies ran while one was open for 9% of the time, Pallas kernels for 0%

profile of v1, /device:TPU:82, one launch (start us, length us, event | category | flops | bytes accessed | tf_op | source)
XLA Modules:
  0.0 655.4 jit_solution(2153268841787886195)
XLA Ops:
  0.7 14.0 %multiply_convert_fusion.1 = (bf16[512,1,1440]{0,2,1:T(8,128)(2,1)S(1)}, bf16[512,1,1440]{0,2,1:T(8,128)(2,1)S(1)}, bf16[512,1,1440]{0,2,1:T(8,128)(2,1)S(1)}, bf16[512,1,1440]{0,2,1:T(8,128)(2,1)S(1)}) fusion(f32[512]{0:T(512)S(1)} %select_multiply_fusion, s32[512]{0:T(512)} %param.6), kind=kLoop, calls=%fused_computation.28 | loop fusion | flops 13271040 | bytes 5902336 | tf_op jit(solution)/shard_map/convert
  14.7 2.9 pad_maximum_fusion
  17.6 7.4 %copy.21 = bf16[512,2,1440]{2,1,0:T(2,128)(2,1)S(1)} copy(bf16[512,2,1440]{0,2,1:T(8,128)(2,1)} %get-tuple-element.27) | data formatting | bytes 5898240 | tf_op jit(solution)/shard_map/stack | solution.py:15
  25.0 3.6 convert_element_type.65
  28.6 11.9 %copy.22 = bf16[16,180,1440]{2,1,0:T(8,128)(2,1)} copy(bf16[16,180,1440]{2,0,1:T(8,128)(2,1)} %param.5) | data formatting | bytes 16588800 | tf_op args[0]
  40.5 10.9 %reshape.233 = bf16[2880,1440]{1,0:T(8,128)(2,1)} reshape(bf16[16,180,1440]{2,1,0:T(8,128)(2,1)} %copy.22) | data formatting | bytes 16588800 | tf_op jit(solution)/shard_map/reshape | solution.py:33
  51.4 13.9 %convolution_convert_fusion.1 = bf16[1024,2880]{0,1:T(8,128)(2,1)} fusion(bf16[1024,1440]{1,0:T(8,128)(2,1)S(1)} %copy-done.2, bf16[2880,1440]{1,0:T(8,128)(2,1)} %reshape.233), kind=kOutput, calls=%fused_computation.17 | convolution fusion | flops 8496414720 | bytes 17141760 | tf_op jit(solution)/shard_map/dot_general | solution.py:31
  65.3 8.5 %copy.23 = bf16[1024,2880]{1,0:T(8,128)(2,1)} copy(bf16[1024,2880]{0,1:T(8,128)(2,1)} %convolution_convert_fusion.1) | data formatting | bytes 11796480 | tf_op jit(solution)/shard_map/convert_element_type | solution.py:37
  73.8 27.5 %reshape.234 = bf16[1,512,2,16,180]{4,3,2,1,0:T(8,128)(2,1)} reshape(bf16[1024,2880]{1,0:T(8,128)(2,1)} %copy.23) | data formatting | bytes 11796480 | tf_op jit(solution)/shard_map/reshape | solution.py:42
  101.3 1.6 constant_dynamic-update-slice_fusion.63
  102.8 1.6 constant_dynamic-update-slice_fusion.62
  106.0 1.6 constant_dynamic-update-slice_fusion.60
  107.5 1.6 constant_dynamic-update-slice_fusion.59
  112.2 1.6 constant_dynamic-update-slice_fusion.56
  116.9 1.6 constant_dynamic-update-slice_fusion.53
  118.4 1.6 constant_dynamic-update-slice_fusion.52
  126.2 1.6 constant_dynamic-update-slice_fusion.47
  132.4 1.6 constant_dynamic-update-slice_fusion.43
  135.6 1.6 constant_dynamic-update-slice_fusion.41
  137.1 1.6 constant_dynamic-update-slice_fusion.40
  144.9 1.6 constant_dynamic-update-slice_fusion.35
  146.5 1.6 constant_dynamic-update-slice_fusion.34
  148.0 1.6 constant_dynamic-update-slice_fusion.33
  149.6 1.6 constant_dynamic-update-slice_fusion.32
  151.2 1.6 constant_dynamic-update-slice_fusion.31
  152.7 1.6 constant_dynamic-update-slice_fusion.30
  155.8 1.6 constant_dynamic-update-slice_fusion.28
  157.4 1.6 constant_dynamic-update-slice_fusion.27
  166.8 1.6 constant_dynamic-update-slice_fusion.21
  168.3 1.6 constant_dynamic-update-slice_fusion.20
  176.1 1.6 constant_dynamic-update-slice_fusion.15
  177.7 1.6 constant_dynamic-update-slice_fusion.14
  180.8 1.6 constant_dynamic-update-slice_fusion.12
  182.4 1.6 constant_dynamic-update-slice_fusion.11
  185.5 1.6 constant_dynamic-update-slice_fusion.9
  188.6 1.6 constant_dynamic-update-slice_fusion.7
  194.8 1.6 constant_dynamic-update-slice_fusion.3
  196.4 1.6 constant_dynamic-update-slice_fusion.2
  198.0 1.6 constant_dynamic-update-slice_fusion.1
  201.1 11.1 %all-to-all-start = ((bf16[64,1,8,2,16,180]{5,4,3,2,1,0:T(8,128)(2,1)}), bf16[64,1,8,2,16,180]{5,4,3,2,1,0:T(8,128)(2,1)}, u32[]{:S(2)}, u32[]{:S(2)}) async-start(bf16[64,1,8,2,16,180]{5,4,3,2,1,0:T(8,128)(2,1)} %constant_dynamic-update-slice_fusion), calls=%async_computation | async-start | bytes 16777216 | tf_op jit(solution)/shard_map/all_to_all | solution.py:39
  213.1 16.2 %while.1 = (s32[]{:T(128)}, f32[1440,256]{1,0:T(8,128)S(1)}, s32[8,2]{0,1:T(2,128)S(1)}, f32[8,720,256]{2,1,0:T(8,128)}, s32[]{:T(128)}) while((s32[]{:T(128)}, f32[1440,256]{1,0:T(8,128)S(1)}, s32[8,2]{0,1:T(2,128)S(1)}, f32[8,720,256]{2,1,0:T(8,128)}, s32[]{:T(128)}) %tuple.21), condition=%wide.while_cond, body=%wide.while_body.sunk | while | flops 2 | bytes 1475673 | solution.py:64
  229.4 13.0 %mul.158 = f32[8,720,2,256]{3,2,1,0:T(2,128)} broadcast(f32[8,720,256]{2,1,0:T(8,128)} %get-tuple-element.12), dimensions={0,1,3} | broadcast | bytes 17694720 | tf_op jit(solution)/shard_map/mul | solution.py:70
  242.4 14.9 %mul.159 = f32[11520,256]{1,0:T(8,128)} reshape(f32[8,720,2,256]{3,2,1,0:T(2,128)} %mul.158) | data formatting | bytes 23592960 | tf_op jit(solution)/shard_map/mul | solution.py:70
  258.8 2.4 broadcast_in_dim.37
  261.3 72.6 %all-to-all-done = bf16[64,1,8,2,16,180]{5,4,3,2,1,0:T(8,128)(2,1)} async-done(((bf16[64,1,8,2,16,180]{5,4,3,2,1,0:T(8,128)(2,1)}), bf16[64,1,8,2,16,180]{5,4,3,2,1,0:T(8,128)(2,1)}, u32[]{:S(2)}, u32[]{:S(2)}) %all-to-all-start) | async-done | bytes 5898272 | tf_op jit(solution)/shard_map/all_to_all | solution.py:39
  333.9 12.1 %copy.43 = bf16[4,16,8,2,16,180]{5,0,4,1,3,2:T(4,128)(2,1)} copy(bf16[4,16,8,2,16,180]{5,4,3,2,1,0:T(8,128)(2,1)} %bitcast.64) | data formatting | bytes 11796480 | tf_op jit(solution)/shard_map/reshape;reshape | solution.py:53
  346.0 15.3 %reshape.235 = bf16[8,512,720]{2,1,0:T(8,128)(2,1)} reshape(bf16[8,2,16,16,4,180]{5,4,3,2,1,0:T(4,128)(2,1)} %bitcast.289) | data formatting | bytes 11796480 | tf_op jit(solution)/shard_map/reshape | solution.py:56
  361.2 14.4 %convolution_bitcast_fusion = f32[8,720,512]{2,1,0:T(8,128)} fusion(bf16[8,512,720]{2,1,0:T(8,128)(2,1)} %reshape.235, bf16[8,720,720]{2,1,0:T(8,128)(2,1)} %param.7), kind=kOutput, calls=%fused_computation.19 | convolution fusion | flops 4246732800 | bytes 25989120 | tf_op jit(solution)/shard_map/sjl,sxl->sjx/dot_general | solution.py:61
  375.7 13.5 %reshape.236 = f32[11520,256]{1,0:T(8,128)} reshape(f32[8,720,512]{2,1,0:T(8,128)} %convolution_bitcast_fusion) | data formatting | bytes 23592960 | tf_op jit(solution)/shard_map/reshape | solution.py:70
  389.2 13.5 %convolution_convert_fusion = bf16[11520,256]{1,0:T(8,128)(2,1)} fusion(bf16[256,256]{1,0:T(8,128)(2,1)S(1)} %copy-done, f32[11520,256]{1,0:T(8,128)} %reshape.236, f32[11520,256]{1,0:T(8,128)} %mul.159, pred[11520]{0:T(1024)(128)(4,1)S(1)} %broadcast_in_dim.37), kind=kOutput, calls=%fused_computation.12 | convolution fusion | flops 1521745920 | bytes 29633792 | tf_op jit(solution)/shard_map/dot_general | solution.py:74
  402.7 9.7 %reshape.237 = bf16[8,720,512]{2,1,0:T(8,128)(2,1)} reshape(bf16[11520,256]{1,0:T(8,128)(2,1)} %convolution_convert_fusion) | data formatting | bytes 11796480 | tf_op jit(solution)/shard_map/reshape | solution.py:77
  412.3 11.8 %convolution_convert_fusion.2 = bf16[8,512,720]{1,2,0:T(8,128)(2,1)} fusion(bf16[8,720,512]{2,1,0:T(8,128)(2,1)} %reshape.237, bf16[8,720,720]{2,1,0:T(8,128)(2,1)} %param.7), kind=kOutput, calls=%fused_computation.20 | convolution fusion | flops 4249681920 | bytes 20090880 | tf_op jit(solution)/shard_map/sjx,sjl->sxl/dot_general | solution.py:78
  424.2 8.4 %copy.27 = bf16[8,512,720]{2,1,0:T(8,128)(2,1)} copy(bf16[8,512,720]{1,2,0:T(8,128)(2,1)} %convolution_convert_fusion.2) | data formatting | bytes 11796480 | tf_op jit(solution)/shard_map/convert_element_type | solution.py:78
  432.6 18.0 %reshape.238 = bf16[8,2,16,16,4,180]{5,4,3,2,1,0:T(4,128)(2,1)} reshape(bf16[8,512,720]{2,1,0:T(8,128)(2,1)} %copy.27) | data formatting | bytes 11796480 | tf_op jit(solution)/shard_map/reshape | solution.py:81
  450.7 8.2 %copy.28 = bf16[4,16,8,2,16,180]{5,4,3,2,1,0:T(8,128)(2,1)} copy(bf16[4,16,8,2,16,180]{5,0,4,1,3,2:T(4,128)(2,1)} %bitcast.290) | data formatting | bytes 11796480 | tf_op jit(solution)/shard_map/transpose | solution.py:81
  458.9 9.6 %all-to-all-start.1 = ((bf16[64,8,2,16,180]{4,3,2,1,0:T(8,128)(2,1)}), bf16[64,8,2,16,180]{4,3,2,1,0:T(8,128)(2,1)}, u32[]{:S(2)}, u32[]{:S(2)}) async-start(bf16[64,8,2,16,180]{4,3,2,1,0:T(8,128)(2,1)} %bitcast.291), calls=%async_computation.1 | async-start | bytes 16777216 | tf_op jit(solution)/shard_map/all_to_all | solution.py:85
  468.5 7.4 %copy.30 = bf16[512,2,1440]{2,1,0:T(2,128)(2,1)S(1)} copy(bf16[512,2,1440]{0,2,1:T(8,128)(2,1)} %get-tuple-element.28) | data formatting | bytes 5898240 | tf_op jit(solution)/shard_map/stack | solution.py:17
  476.0 3.5 convert_element_type.70
  479.5 111.9 %all-to-all-done.1 = bf16[64,8,2,16,180]{4,3,2,1,0:T(8,128)(2,1)} async-done(((bf16[64,8,2,16,180]{4,3,2,1,0:T(8,128)(2,1)}), bf16[64,8,2,16,180]{4,3,2,1,0:T(8,128)(2,1)}, u32[]{:S(2)}, u32[]{:S(2)}) %all-to-all-start.1) | async-done | bytes 5898272 | tf_op jit(solution)/shard_map/all_to_all | solution.py:85
  591.4 15.6 %reshape.240 = bf16[1024,2880]{1,0:T(8,128)(2,1)} reshape(bf16[64,8,2,16,180]{4,3,2,1,0:T(8,128)(2,1)} %all-to-all-done.1) | data formatting | bytes 11796480 | tf_op jit(solution)/shard_map/reshape | solution.py:86
  607.0 8.4 %copy.29 = bf16[2880,1024]{1,0:T(8,128)(2,1)} copy(bf16[2880,1024]{0,1:T(8,128)(2,1)} %bitcast.292) | data formatting | bytes 11796480 | tf_op jit(solution)/shard_map/dot_general | solution.py:87
  615.4 8.0 %dot_general.27 = bf16[16,180,1024]{2,1,0:T(8,128)(2,1)} reshape(bf16[2880,1024]{1,0:T(8,128)(2,1)} %copy.29) | data formatting | bytes 11796480 | tf_op jit(solution)/shard_map/dot_general | solution.py:87
  623.4 16.3 %fusion.11 = f32[16,180,1440]{2,1,0:T(8,128)} fusion(bf16[16,180,1024]{2,1,0:T(8,128)(2,1)} %dot_general.27, bf16[1024,1440]{1,0:T(8,128)(2,1)} %convert_element_type.70), kind=kOutput, calls=%fused_computation.21 | convolution fusion | flops 8493465600 | bytes 25436160 | tf_op jit(solution)/shard_map/dot_general | solution.py:87
  639.7 15.3 %fusion.8 = bf16[16,180,1440]{2,0,1:T(8,128)(2,1)} fusion(f32[16,180,1440]{2,1,0:T(8,128)} %fusion.11, bf16[16,180,1440]{2,0,1:T(8,128)(2,1)S(1)} %bitcast.288), kind=kLoop, calls=%fused_computation.11 | loop fusion | flops 45619200 | bytes 33177600 | tf_op jit(solution)/shard_map/convert_element_type | solution.py:94
  (80 shorter events, 72.2 us)
Async XLA Ops:
  0.0 389.2 %copy-start = (bf16[256,256]{1,0:T(8,128)(2,1)S(1)}, bf16[256,256]{1,0:T(8,128)(2,1)}, u32[]{:S(2)}) copy-start(bf16[256,256]{1,0:T(8,128)(2,1)} %param.9) | copy-start | bytes 393220
  40.5 10.9 %copy-start.2 = (bf16[1024,1440]{1,0:T(8,128)(2,1)S(1)}, bf16[1024,1440]{1,0:T(8,128)(2,1)}, u32[]{:S(2)}) copy-start(bf16[1024,1440]{1,0:T(8,128)(2,1)} %convert_element_type.65) | copy-start | bytes 8847364
  201.1 11.9 %copy-start.3 = (f32[720,256]{1,0:T(8,128)S(1)}, f32[720,256]{1,0:T(8,128)}, u32[]{:S(2)}) copy-start(f32[720,256]{1,0:T(8,128)} %param.8) | copy-start | bytes 2211844
  201.1 132.7 %all-to-all-start = ((bf16[64,1,8,2,16,180]{5,4,3,2,1,0:T(8,128)(2,1)}), bf16[64,1,8,2,16,180]{5,4,3,2,1,0:T(8,128)(2,1)}, u32[]{:S(2)}, u32[]{:S(2)}) async-start(bf16[64,1,8,2,16,180]{5,4,3,2,1,0:T(8,128)(2,1)} %constant_dynamic-update-slice_fusion), calls=%async_computation | async-start | bytes 16777216 | tf_op jit(solution)/shard_map/all_to_all | solution.py:39
  458.9 132.5 %all-to-all-start.1 = ((bf16[64,8,2,16,180]{4,3,2,1,0:T(8,128)(2,1)}), bf16[64,8,2,16,180]{4,3,2,1,0:T(8,128)(2,1)}, u32[]{:S(2)}, u32[]{:S(2)}) async-start(bf16[64,8,2,16,180]{4,3,2,1,0:T(8,128)(2,1)} %bitcast.291), calls=%async_computation.1 | async-start | bytes 16777216 | tf_op jit(solution)/shard_map/all_to_all | solution.py:85
  615.4 24.3 %slice-start = ((s8[8847360]{0:T(1024)(128)(4,1)}), s8[458752]{0:T(1024)(128)(4,1)S(1)}, s32[]{:S(2)}) async-start(s8[8847360]{0:T(1024)(128)(4,1)} %bitcast.287), calls=%async_computation.2 | async-start | bytes 917504
  623.4 16.3 %slice-start.1 = ((s8[8847360]{0:T(1024)(128)(4,1)}), s8[4194304]{0:T(1024)(128)(4,1)S(1)}, s32[]{:S(2)}) async-start(s8[8847360]{0:T(1024)(128)(4,1)} %bitcast.287), calls=%async_computation.3 | async-start | bytes 8388608
  623.4 16.3 %slice-start.2 = ((s8[8847360]{0:T(1024)(128)(4,1)}), s8[4194304]{0:T(1024)(128)(4,1)S(1)}, s32[]{:S(2)}) async-start(s8[8847360]{0:T(1024)(128)(4,1)} %bitcast.287), calls=%async_computation.4 | async-start | bytes 8388608
  639.7 15.3 %copy-start.1 = (bf16[256,256]{1,0:T(8,128)(2,1)S(1)}, bf16[256,256]{1,0:T(8,128)(2,1)}, u32[]{:S(2)}) copy-start(bf16[256,256]{1,0:T(8,128)(2,1)} %param.9) | copy-start | bytes 393220
